TPU v7x, 32 devices: a whole 2x2x4 slice. The times are simulated.
32 devices in a mesh: grp: 4 (over x, core), tile: 8 (over z, y).
Axes of the slice: x: 2, y: 2, z: 4, core: 2. Of those that a mesh axis runs over, the one named last changes fastest.
Arguments:
- start_block: float32 [65536, 256], P(('grp', 'tile')), may hold values from -8 to 8
- dense_tiles: float32 [32, 2048, 2048], P(('grp', 'tile')), as said below
- basis: float32 [32, 48, 2048], P(('grp', 'tile')), may hold values from -0.125 to 0.125
- coupling: float32 [4, 8, 48, 1536], P(None, 'tile', None, 'grp'), as said below
- admissible: int32 [4, 8, 32], P(None, 'tile', 'grp'), may hold values from 0 to 1, as said below
Outputs:
- modes: float32 [65536, 256], P(('grp', 'tile'))
Inputs may be any that keep to these rules, and one draw needn't show every extreme that they name: admissible is symmetric over tile pairs (the entry for row tile i and column tile j equals that for row tile j and column tile i) and 0 where the row tile equals the column tile. `dense_tiles`: each dense tile is symmetric: a positive scale times a diagonal plus an unstructured symmetric off-diagonal part. The coupling, read as a matrix of order 32 * 48, is symmetric: block S_ji is the transpose of S_ij.
All inputs are finite; a program needn't handle non-finite values.
Results may differ from a plain program's by a relative error of at most 0.0003.
Values sent between devices are 32-bit elements; how exact they have to be, the bound alone decides.
No kernel may reach another device: no remote copies, remote signals or barrier semaphores. Data moves between devices by JAX's collectives and lax.ppermute only.
A program may use at most 128 MiB of HBM per device.

v0:
```python
import jax
import jax.numpy as jnp
from jax import lax
from jax.sharding import PartitionSpec as P


def body(start_block, dense_tiles, basis, coupling, admissible):
    hp = lax.Precision.HIGHEST
    groups = coupling.shape[0]
    width = basis.shape[1]
    span = coupling.shape[3] // width
    modes_count = start_block.shape[1]
    flags = admissible.astype(jnp.float32).reshape(groups, 1, span, 1)
    masked = (coupling.reshape(groups, width, span, width) * flags).reshape(
        groups * width, span * width
    )
    dense = dense_tiles[0]
    rows_basis = basis[0]
    total_rows = lax.axis_size("grp") * lax.axis_size("tile") * start_block.shape[0]

    def add_columns(piece):
        return jnp.dot(masked, piece, precision=hp, preferred_element_type=jnp.float32)

    def apply_operator(field):
        coeffs = jnp.dot(rows_basis, field, precision=hp)
        partial_rows = add_columns(lax.all_gather(coeffs, "tile", axis=0, tiled=True))
        summed = lax.psum_scatter(
            partial_rows.reshape(groups, width, modes_count), "grp", scatter_dimension=0, tiled=True
        )[0]
        far = lax.dot_general(rows_basis, summed, (((0,), (0,)), ((), ())), precision=hp)
        near = jnp.dot(dense, field, precision=hp)
        return far + near

    def whitening(field):
        local_gram = lax.dot_general(field, field, (((0,), (0,)), ((), ())), precision=hp)
        gram = lax.psum(local_gram, ("grp", "tile")) / jnp.float32(total_rows)
        lower = jnp.linalg.cholesky(gram)
        return lax.linalg.triangular_solve(
            lower, jnp.eye(modes_count, dtype=gram.dtype), left_side=True, lower=True
        )

    image = apply_operator(start_block)
    inverse = whitening(image)
    further = apply_operator(image)
    image = jnp.dot(further, inverse.T, precision=hp)
    inverse = whitening(image)
    return jnp.dot(image, inverse.T, precision=hp)


def solution(mesh):
    placed = (
        P(("grp", "tile"), None),
        P(("grp", "tile"), None, None),
        P(("grp", "tile"), None, None),
        P(None, "tile", None, "grp"),
        P(None, "tile", "grp"),
    )
    return jax.shard_map(
        body, mesh=mesh, in_specs=placed, out_specs=P(("grp", "tile"), None), check_vma=False
    )
```

profile of v0, /device:TPU:0, one launch (start us, length us, event | category | flops | bytes accessed | tf_op | source)
XLA Modules:
  0.0 498.3 jit_solution(8622387900580312000)
XLA Ops:
  8.1 2.1 fusion.19
  10.3 32.8 %all_gather.6 = f32[384,256]{1,0:T(8,128)S(1)} all-gather(f32[48,256]{1,0:T(8,128)S(1)} %fusion.19), channel_id=1, replica_groups=mesh['grp'=4,'tile'=8] {'tile'}, dimensions={0}, use_global_device_ids=true | all-gather | bytes 442368 | tf_op jit(solution)/shard_map/all_gather | solution.py:26
  44.3 18.6 %fusion.2 = f32[2048,256]{0,1:T(8,128)} fusion(f32[2048,256]{1,0:T(8,128)S(1)} %copy-done, f32[1,2048,2048]{2,1,0:T(8,128)} %param.9), kind=kOutput, calls=%fused_computation.6 | convolution fusion | flops 12884901888 | bytes 20971520 | tf_op jit(solution)/shard_map/dot_general | solution.py:31
  62.9 2.4 reduce-scatter.3.cloned.1.call-done
  65.3 2.8 convolution_bitcast_fusion
  68.1 1.3 copy-done.3
  69.4 2.7 fusion.4
  72.1 4.3 fusion.9
  76.5 18.3 %fusion = f32[256,2048]{1,0:T(8,128)} fusion(f32[1,2048,2048]{2,1,0:T(8,128)} %param.9, f32[2048,256]{0,1:T(8,128)S(1)} %copy-done.4, f32[2048,256]{0,1:T(8,128)S(1)} %copy-done.2), kind=kOutput, calls=%fused_computation.4 | convolution fusion | flops 12885426176 | bytes 23068672 | tf_op jit(solution)/shard_map/dot_general | solution.py:31
  94.9 31.3 %all_gather.7 = f32[384,256]{1,0:T(8,128)S(1)} all-gather(f32[48,256]{1,0:T(8,128)S(1)} %fusion.9), channel_id=1, replica_groups=mesh['grp'=4,'tile'=8] {'tile'}, dimensions={0}, use_global_device_ids=true | all-gather | bytes 442368 | tf_op jit(solution)/shard_map/all_gather | solution.py:26
  126.2 1.2 fusion.12
  127.5 94.4 %all-reduce.4.cloned.1.call-done = f32[256,256]{0,1:T(8,128)} async-done(((f32[256,256]{0,1:T(8,128)}), f32[256,256]{0,1:T(8,128)}) %all-reduce.4.cloned.1.call-update) | async-done | bytes 262160 | tf_op jit(solution)/shard_map/psum | solution.py:36
  224.0 11.7 %cholesky.130 = f32[128,128]{1,0:T(8,128)S(1)} custom-call(f32[128,128]{1,0:T(8,128)S(1)} %cholesky.194), custom_call_target="Cholesky" | custom-call | tf_op jit(solution)/shard_map/jit(cholesky)/cholesky | solution.py:37
  235.8 9.8 %custom-call.13 = f32[1,128,128]{1,2,0:T(8,128)S(1)} custom-call(f32[1,128,128]{2,1,0:T(8,128)S(1)} %get-tuple-element.50), custom_call_target="InvertDiagBlocksLowerTriangular" | custom-call | tf_op jit(solution)/shard_map/jit(cholesky)/cholesky | solution.py:37
  246.1 11.7 %cholesky.147 = f32[128,128]{1,0:T(8,128)S(1)} custom-call(f32[128,128]{1,0:T(8,128)S(1)} %convolution_subtract_fusion.3), custom_call_target="Cholesky" | custom-call | tf_op jit(solution)/shard_map/jit(cholesky)/cholesky | solution.py:37
  259.9 4.1 while.4
  260.6 1.3 bitcast_dynamic-update-slice_fusion.4
  262.7 1.3 bitcast_dynamic-update-slice_fusion.4
  264.0 20.1 %custom-call.14 = f32[2,128,128]{1,2,0:T(8,128)S(1)} custom-call(f32[2,128,128]{2,1,0:T(8,128)S(1)} %get-tuple-element.21), custom_call_target="InvertDiagBlocksLowerTriangular" | custom-call | tf_op jit(solution)/shard_map/triangular_solve/custom-call.0 | solution.py:38
  285.0 3.5 convolution_add_fusion
  288.6 3.6 fusion.21
  292.2 1.3 copy-done.5
  293.5 4.3 fusion.54
  297.8 125.8 %all-reduce.6.cloned.1.call-done = f32[256,256]{0,1:T(8,128)} async-done(((f32[256,256]{0,1:T(8,128)}), f32[256,256]{0,1:T(8,128)}) %all-reduce.6.cloned.1.call-update) | async-done | bytes 262160 | tf_op jit(solution)/shard_map/psum | solution.py:36
  425.7 11.9 %cholesky.164 = f32[128,128]{1,0:T(8,128)S(1)} custom-call(f32[128,128]{1,0:T(8,128)S(1)} %cholesky.197), custom_call_target="Cholesky" | custom-call | tf_op jit(solution)/shard_map/jit(cholesky)/cholesky | solution.py:37
  437.6 9.8 %custom-call.15 = f32[1,128,128]{1,2,0:T(8,128)S(1)} custom-call(f32[1,128,128]{2,1,0:T(8,128)S(1)} %get-tuple-element.46), custom_call_target="InvertDiagBlocksLowerTriangular" | custom-call | tf_op jit(solution)/shard_map/jit(cholesky)/cholesky | solution.py:37
  447.9 11.7 %cholesky.181 = f32[128,128]{1,0:T(8,128)S(1)} custom-call(f32[128,128]{1,0:T(8,128)S(1)} %convolution_subtract_fusion.2), custom_call_target="Cholesky" | custom-call | tf_op jit(solution)/shard_map/jit(cholesky)/cholesky | solution.py:37
  462.3 3.9 while.5
  462.9 1.4 bitcast_dynamic-update-slice_fusion.5
  464.9 1.4 bitcast_dynamic-update-slice_fusion.5
  466.2 19.7 %custom-call.16 = f32[2,128,128]{1,2,0:T(8,128)S(1)} custom-call(f32[2,128,128]{2,1,0:T(8,128)S(1)} %get-tuple-element.22), custom_call_target="InvertDiagBlocksLowerTriangular" | custom-call | tf_op jit(solution)/shard_map/triangular_solve/custom-call.0 | solution.py:38
  486.8 4.7 fusion.25
  (69 shorter events, 14.8 us)
Async XLA Ops:
  6.5 1.6 copy-start
  6.5 36.5 %copy-start.7 = (f32[4,1,48,384]{3,2,1,0:T(8,128)S(1)}, f32[4,1,48,384]{3,2,1,0:T(8,128)}, u32[]{:S(2)}) copy-start(f32[4,1,48,384]{3,2,1,0:T(8,128)} %param.11) | copy-start | bytes 884740
  6.5 58.7 %reduce-scatter.3.cloned.1.call-start = ((), (), s32[]{:S(2)}) async-start(), calls=%async_computation.2 | async-start | bytes 245760 | tf_op jit(solution)/shard_map/reduce_scatter | solution.py:27
  44.2 21.0 %copy-start.6 = (f32[1,48,2048]{2,1,0:T(8,128)S(1)}, f32[1,48,2048]{2,1,0:T(8,128)}, u32[]{:S(2)}) copy-start(f32[1,48,2048]{2,1,0:T(8,128)} %param.10) | copy-start | bytes 1179652
  44.2 177.7 %all-reduce.4.cloned.1.call-start = ((), (), s32[]{:S(2)}) async-start(), calls=%async_computation.4 | async-start | bytes 524288 | tf_op jit(solution)/shard_map/psum | solution.py:36
  65.3 4.1 copy-start.1
  68.1 1.3 copy-start.3
  72.1 4.3 copy-start.2
  72.1 4.4 copy-start.4
  94.8 190.2 %reduce-scatter.5.cloned.1.call-start = ((), (), s32[]{:S(2)}) async-start(), calls=%async_computation.3 | async-start | bytes 245760 | tf_op jit(solution)/shard_map/reduce_scatter | solution.py:27
  127.4 296.2 %all-reduce.6.cloned.1.call-start = ((), (), s32[]{:S(2)}) async-start(), calls=%async_computation.5 | async-start | bytes 524288 | tf_op jit(solution)/shard_map/psum | solution.py:36
  292.1 1.4 copy-start.5
Sparse Core Ops, SparseCore 0:
  44.4 20.8 reduce-scatter.2
  95.0 126.9 all-reduce.3
  224.4 18.9 reduce-scatter.4
  298.0 125.6 all-reduce.5
where the time goes:
time: 506 us; the launch traced here: 498 us
  waiting for transfers between devices  223 us (44%)
  other arithmetic  113 us (22%)
  matrix products  70.1 us (14%)
  blocking collectives  64.1 us (13%)
  between operations  16.1 us (3%)
  local copies, waits for them, and re-layouts  11.8 us (2%)
    psum x2, waiting for transfers between devices, whitening(): gram = lax.psum(local_gram, ('grp', 'tile')) / jnp.float32(total_rows)  220 us
    another operation x13, other arithmetic, whitening(): lower = jnp.linalg.cholesky(gram)  68.8 us
    all_gather x2, blocking collectives, apply_operator(): lax.all_gather(coeffs, 'tile', axis=0, tiled=True)  64.1 us
    another operation x5, other arithmetic, whitening(): lax.linalg.triangular_solve(lower, jnp.eye(modes_count, dtype=gram.dtype)...  39.8 us
    dot_general x2, matrix products, apply_operator(): near = jnp.dot(dense, field, precision=hp)  36.9 us
  transfers between devices with their start and end apart: 4, of which 3 were waited for; matrix products, arithmetic and copies ran while one was open for 16% of the time, Pallas kernels for 0%

commit v1 on v0

--- a/solution.py
+++ b/solution.py
@@ -33,7 +33,9 @@
 
     def whitening(field):
         local_gram = lax.dot_general(field, field, (((0,), (0,)), ((), ())), precision=hp)
-        gram = lax.psum(local_gram, ("grp", "tile")) / jnp.float32(total_rows)
+        gram = jnp.sum(lax.all_gather(local_gram, ("grp", "tile")), axis=0) / jnp.float32(
+            total_rows
+        )
         lower = jnp.linalg.cholesky(gram)
         return lax.linalg.triangular_solve(
             lower, jnp.eye(modes_count, dtype=gram.dtype), left_side=True, lower=True

time: 506 us -> 450 us (0.89)
  waiting for transfers between devices: 223 us -> 147 us
  other arithmetic: 113 us -> 127 us
    psum x2 -> x0, waiting for transfers between devices: 220 us -> none  [whitening(): gram = lax.psum(local_gram, ('grp', 'tile')) / jnp.float32(total_rows)]
    all_gather x0 -> x2, waiting for transfers between devices: none -> 145 us  [whitening(): lax.all_gather(local_gram, ('grp', 'tile'))]
    another operation x13, other arithmetic: 68.8 us -> 79.2 us  [whitening(): lower = jnp.linalg.cholesky(gram)]
    reduce_sum x0 -> x2, other arithmetic: none -> 7.86 us  [whitening(): jnp.sum(lax.all_gather(local_gram, ('grp', 'tile')), axis=0)]
  transfers between devices with their start and end apart: 4 -> 4, of which waited for: 3 -> 3; matrix products, arithmetic and copies ran while one was open for 16% -> 11% of each run, Pallas kernels for 0% -> 0%
where the time goes in v1:
time: 450 us; the launch traced here: 442 us
  waiting for transfers between devices  147 us (33%)
  other arithmetic  127 us (28%)
  matrix products  75.1 us (17%)
  blocking collectives  64 us (14%)
  between operations  16.4 us (4%)
  local copies, waits for them, and re-layouts  11.8 us (3%)
    all_gather x2, waiting for transfers between devices, whitening(): lax.all_gather(local_gram, ('grp', 'tile'))  145 us
    another operation x13, other arithmetic, whitening(): lower = jnp.linalg.cholesky(gram)  79.2 us
    all_gather x2, blocking collectives, apply_operator(): lax.all_gather(coeffs, 'tile', axis=0, tiled=True)  64 us
    another operation x5, other arithmetic, whitening(): lax.linalg.triangular_solve(lower, jnp.eye(modes_count, dtype=gram.dtype)...  39.4 us
    dot_general x2, matrix products, apply_operator(): near = jnp.dot(dense, field, precision=hp)  37.9 us
    dot_general x2, matrix products, whitening(): lax.dot_general(field, field, (((0,), (0,)), ((), ())), precision=hp)  10.6 us
  transfers between devices with their start and end apart: 4, of which 3 were waited for; matrix products, arithmetic and copies ran while one was open for 11% of the time, Pallas kernels for 0%

profile of v1, /device:TPU:0, one launch (start us, length us, event | category | flops | bytes accessed | tf_op | source)
XLA Modules:
  0.0 441.8 jit_solution(3478250483609635464)
XLA Ops:
  6.5 1.6 copy-done
  8.1 2.1 fusion.19
  10.2 32.8 %all_gather.18 = f32[384,256]{1,0:T(8,128)S(1)} all-gather(f32[48,256]{1,0:T(8,128)S(1)} %fusion.19), channel_id=1, replica_groups=mesh['grp'=4,'tile'=8] {'tile'}, dimensions={0}, use_global_device_ids=true | all-gather | bytes 442368 | tf_op jit(solution)/shard_map/all_gather | solution.py:26
  44.4 18.6 %fusion.2 = f32[2048,256]{0,1:T(8,128)} fusion(f32[2048,256]{1,0:T(8,128)S(1)} %copy-done, f32[1,2048,2048]{2,1,0:T(8,128)} %param.9), kind=kOutput, calls=%fused_computation.6 | convolution fusion | flops 12884901888 | bytes 20971520 | tf_op jit(solution)/shard_map/dot_general | solution.py:31
  63.0 2.4 reduce-scatter.3.cloned.1.call-done
  65.4 2.8 convolution_bitcast_fusion
  68.2 2.0 fusion.9
  70.2 31.3 %all_gather.19 = f32[384,256]{1,0:T(8,128)S(1)} all-gather(f32[48,256]{1,0:T(8,128)S(1)} %fusion.9), channel_id=1, replica_groups=mesh['grp'=4,'tile'=8] {'tile'}, dimensions={0}, use_global_device_ids=true | all-gather | bytes 442368 | tf_op jit(solution)/shard_map/all_gather | solution.py:26
  102.7 6.3 %fusion.4 = f32[256,256]{1,0:T(8,128)} fusion(f32[2048,256]{0,1:T(8,128)} %copy-done.2, f32[2048,256]{0,1:T(8,128)} %fusion.2), kind=kOutput, calls=%fused_computation.8 | convolution fusion | flops 1611137024 | bytes 4456448 | tf_op jit(solution)/shard_map/dot_general | solution.py:35
  109.3 19.4 %fusion = f32[256,2048]{1,0:T(8,128)} fusion(f32[1,2048,2048]{2,1,0:T(8,128)} %param.9, f32[2048,256]{0,1:T(8,128)} %copy-done.2, f32[2048,256]{0,1:T(8,128)} %fusion.2), kind=kOutput, calls=%fused_computation.4 | convolution fusion | flops 12885426176 | bytes 23068672 | tf_op jit(solution)/shard_map/dot_general | solution.py:31
  128.7 4.8 %convolution_add_fusion = f32[256,2048]{1,0:T(8,128)} fusion(f32[256,2048]{1,0:T(8,128)} %fusion, f32[1,48,2048]{2,1,0:T(8,128)S(1)} %copy-done.4, f32[1,48,256]{2,1,0:T(8,128)} %reduce-scatter.5.cloned.1.call-done), kind=kOutput, calls=%fused_computation.13 | convolution fusion | flops 302514176 | bytes 4636672 | tf_op jit(solution)/shard_map/dot_general | solution.py:30
  133.4 69.0 %all-gather.5.cloned.1.call-done = f32[8192,256]{1,0:T(8,128)} async-done(((f32[256,256]{1,0:T(8,128)}), f32[8192,256]{1,0:T(8,128)}) %all-gather.5.cloned.1.call-update) | async-done | bytes 8388624 | tf_op jit(solution)/shard_map/all_gather | solution.py:36
  202.5 3.9 reduce_sum.18
  206.8 11.7 %cholesky.130 = f32[128,128]{1,0:T(8,128)S(1)} custom-call(f32[128,128]{1,0:T(8,128)S(1)} %cholesky.194), custom_call_target="Cholesky" | custom-call | tf_op jit(solution)/shard_map/jit(cholesky)/cholesky | solution.py:39
  218.5 9.8 %custom-call.13 = f32[1,128,128]{1,2,0:T(8,128)S(1)} custom-call(f32[1,128,128]{2,1,0:T(8,128)S(1)} %get-tuple-element.50), custom_call_target="InvertDiagBlocksLowerTriangular" | custom-call | tf_op jit(solution)/shard_map/jit(cholesky)/cholesky | solution.py:39
  228.8 22.0 %cholesky.147 = f32[128,128]{1,0:T(8,128)S(1)} custom-call(f32[128,128]{1,0:T(8,128)S(1)} %convolution_subtract_fusion.3), custom_call_target="Cholesky" | custom-call | tf_op jit(solution)/shard_map/jit(cholesky)/cholesky | solution.py:39
  253.0 4.1 while.4
  255.7 1.3 bitcast_dynamic-update-slice_fusion.4
  257.1 19.7 %custom-call.14 = f32[2,128,128]{1,2,0:T(8,128)S(1)} custom-call(f32[2,128,128]{2,1,0:T(8,128)S(1)} %get-tuple-element.21), custom_call_target="InvertDiagBlocksLowerTriangular" | custom-call | tf_op jit(solution)/shard_map/triangular_solve/custom-call.0 | solution.py:40
  277.7 5.2 %fusion.21 = f32[2048,256]{1,0:T(8,128)S(1)} fusion(f32[256,2048]{1,0:T(8,128)} %convolution_add_fusion, f32[128,256]{1,0:T(8,128)S(1)} %fusion.43, f32[128,256]{1,0:T(8,128)S(1)} %fusion.36), kind=kOutput, calls=%fused_computation.32 | convolution fusion | flops 1610678272 | bytes 4456448 | tf_op jit(solution)/shard_map/dot_general | solution.py:47
  282.9 1.4 copy-done.3
  284.2 4.3 fusion.54
  288.6 75.9 %all-gather.7.cloned.1.call-done = f32[8192,256]{1,0:T(8,128)} async-done(((f32[256,256]{1,0:T(8,128)}), f32[8192,256]{1,0:T(8,128)}) %all-gather.7.cloned.1.call-update) | async-done | bytes 8388624 | tf_op jit(solution)/shard_map/all_gather | solution.py:36
  364.5 3.9 reduce_sum.19
  368.8 11.9 %cholesky.164 = f32[128,128]{1,0:T(8,128)S(1)} custom-call(f32[128,128]{1,0:T(8,128)S(1)} %cholesky.197), custom_call_target="Cholesky" | custom-call | tf_op jit(solution)/shard_map/jit(cholesky)/cholesky | solution.py:39
  380.8 9.8 %custom-call.15 = f32[1,128,128]{1,2,0:T(8,128)S(1)} custom-call(f32[1,128,128]{2,1,0:T(8,128)S(1)} %get-tuple-element.46), custom_call_target="InvertDiagBlocksLowerTriangular" | custom-call | tf_op jit(solution)/shard_map/jit(cholesky)/cholesky | solution.py:39
  391.0 11.7 %cholesky.181 = f32[128,128]{1,0:T(8,128)S(1)} custom-call(f32[128,128]{1,0:T(8,128)S(1)} %convolution_subtract_fusion.2), custom_call_target="Cholesky" | custom-call | tf_op jit(solution)/shard_map/jit(cholesky)/cholesky | solution.py:39
  405.5 4.1 while.5
  406.1 1.4 bitcast_dynamic-update-slice_fusion.5
  408.1 1.4 bitcast_dynamic-update-slice_fusion.5
  409.6 19.7 %custom-call.16 = f32[2,128,128]{1,2,0:T(8,128)S(1)} custom-call(f32[2,128,128]{2,1,0:T(8,128)S(1)} %get-tuple-element.22), custom_call_target="InvertDiagBlocksLowerTriangular" | custom-call | tf_op jit(solution)/shard_map/triangular_solve/custom-call.0 | solution.py:40
  430.2 4.7 %fusion.25 = f32[2048,256]{1,0:T(8,128)} fusion(f32[2048,256]{1,0:T(8,128)} %copy-done.3, f32[128,256]{1,0:T(8,128)S(1)} %fusion.39, f32[128,256]{1,0:T(8,128)S(1)} %fusion.34), kind=kOutput, calls=%fused_computation.36 | convolution fusion | flops 1610678272 | bytes 4456448 | tf_op jit(solution)/shard_map/dot_general | solution.py:49
  (71 shorter events, 12.6 us)
Async XLA Ops:
  6.5 1.6 copy-start
  6.5 36.5 %copy-start.6 = (s32[4,1,8]{2,1,0:T(1,128)S(1)}, s32[4,1,8]{2,1,0:T(1,128)}, u32[]{:S(2)}) copy-start(s32[4,1,8]{2,1,0:T(1,128)} %param.12) | copy-start | bytes 388
  6.5 36.6 %copy-start.5 = (f32[4,1,48,384]{3,2,1,0:T(8,128)S(1)}, f32[4,1,48,384]{3,2,1,0:T(8,128)}, u32[]{:S(2)}) copy-start(f32[4,1,48,384]{3,2,1,0:T(8,128)} %param.11) | copy-start | bytes 884740
  6.5 58.8 %reduce-scatter.3.cloned.1.call-start = ((), (), s32[]{:S(2)}) async-start(), calls=%async_computation.2 | async-start | bytes 245760 | tf_op jit(solution)/shard_map/reduce_scatter | solution.py:27
  44.4 21.0 %copy-start.4 = (f32[1,48,2048]{2,1,0:T(8,128)S(1)}, f32[1,48,2048]{2,1,0:T(8,128)}, u32[]{:S(2)}) copy-start(f32[1,48,2048]{2,1,0:T(8,128)} %param.10) | copy-start | bytes 1179652
  44.4 84.3 %reduce-scatter.5.cloned.1.call-start = ((), (), s32[]{:S(2)}) async-start(), calls=%async_computation.3 | async-start | bytes 245760 | tf_op jit(solution)/shard_map/reduce_scatter | solution.py:27
  65.4 2.8 copy-start.1
  68.2 2.0 copy-start.2
  102.6 99.8 %all-gather.5.cloned.1.call-start = ((), (), s32[]{:S(2)}) async-start(), calls=%async_computation.4 | async-start | bytes 8650752 | tf_op jit(solution)/shard_map/all_gather | solution.py:36
  109.0 255.5 %all-gather.7.cloned.1.call-start = ((), (), s32[]{:S(2)}) async-start(), calls=%async_computation.5 | async-start | bytes 8650752 | tf_op jit(solution)/shard_map/all_gather | solution.py:36
  282.8 1.4 copy-start.3
Sparse Core Ops, SparseCore 0:
  44.5 20.8 reduce-scatter.2
  102.8 19.5 reduce-scatter.4
  125.4 77.0 all-gather.4
  288.7 75.7 all-gather.6
